TPU v7x, 32 devices: a whole 2x2x4 slice. The times are simulated.
32 devices in a mesh: dev: 32 (over z, y, x, core).
Axes of the slice: x: 2, y: 2, z: 4, core: 2. Of those that a mesh axis runs over, the one named last changes fastest.
Arguments:
- image_feats: bfloat16 [384, 1152], P('dev'), may hold values from -0.1875 to 0.1875
- text_feats: bfloat16 [384, 1152], P('dev'), may hold values from -0.1875 to 0.1875
- image_head: bfloat16 [1152, 640], replicated, may hold values from -0.1875 to 0.1875
- text_head: bfloat16 [1152, 640], replicated, may hold values from -0.1875 to 0.1875
- log_scale: float32 [], replicated, may hold values from 1.6 to 2.3
- logit_bias: float32 [], replicated, may hold values from -8 to -4
- image_group: int32 [384], P('dev'), may hold values from 0 to 191
- text_group: int32 [384], P('dev'), may hold values from 0 to 191
Outputs:
- loss: float32 [], replicated
- grad_images: bfloat16 [384, 1152], P('dev')
- grad_texts: bfloat16 [384, 1152], P('dev')
- grad_scale: float32 [], replicated
- grad_bias: float32 [], replicated
All inputs are finite; a program needn't handle non-finite values.
Results may differ from a plain program's by a relative error of at most 0.0063.
Values may be sent and summed in bfloat16 or wider, within the bound.
No kernel may reach another device: no remote copies, remote signals or barrier semaphores. Data moves between devices by JAX's collectives and lax.ppermute only.
A program may use at most 128 MiB of HBM per device.

v0:
```python
import jax
import jax.numpy as jnp
from jax import lax
from jax.sharding import PartitionSpec as P

epsilon = 1e-06


def normalize(projected):
    length = jnp.sqrt(jnp.sum(projected * projected, axis=1, keepdims=True) + epsilon)
    return (projected / length, length)


def backward_rows(grad_unit, unit_vec, length, weights):
    inner = jnp.sum(unit_vec * grad_unit, axis=1, keepdims=True)
    grad_proj = ((grad_unit - unit_vec * inner) / length).astype(jnp.bfloat16)
    result = lax.dot_general(
        grad_proj, weights, (((1,), (1,)), ((), ())), preferred_element_type=jnp.float32
    )
    return result.astype(jnp.bfloat16)


def on_device(
    image_feats, text_feats, image_head, text_head, log_scale, logit_bias, image_group, text_group
):
    img_unit, img_length = normalize(
        jnp.dot(image_feats, image_head, preferred_element_type=jnp.float32)
    )
    txt_unit, txt_length = normalize(
        jnp.dot(text_feats, text_head, preferred_element_type=jnp.float32)
    )
    img_emb = img_unit.astype(jnp.bfloat16)
    txt_emb = txt_unit.astype(jnp.bfloat16)
    logit_scale = jnp.exp(log_scale)
    pairs = image_feats.shape[0] * lax.axis_size("dev")
    stacked_emb = jnp.stack([img_emb, txt_emb])
    stacked_ids = jnp.stack([image_group, text_group])
    emb_piece = lax.all_gather(stacked_emb, "dev", axis=1, tiled=True)
    id_piece = lax.all_gather(stacked_ids, "dev", axis=1, tiled=True)
    cap_emb = emb_piece[1]
    cosine = lax.dot_general(
        img_emb, cap_emb, (((1,), (1,)), ((), ())), preferred_element_type=jnp.float32
    )
    label_sign = jnp.where(image_group[:, None] == id_piece[1][None, :], 1.0, -1.0).astype(
        jnp.float32
    )
    margin = label_sign * (logit_scale * cosine + logit_bias)
    slopes = -label_sign * jax.nn.sigmoid(-margin)
    grad_img = logit_scale * jnp.dot(
        slopes.astype(jnp.bfloat16), cap_emb, preferred_element_type=jnp.float32
    )
    added = jnp.stack(
        [jnp.sum(jax.nn.softplus(-margin)), jnp.sum(slopes * cosine), jnp.sum(slopes)]
    )
    caption_side = (grad_img, added)
    img_piece = emb_piece[0]
    cosine = lax.dot_general(
        img_piece, txt_emb, (((1,), (1,)), ((), ())), preferred_element_type=jnp.float32
    )
    label_sign = jnp.where(id_piece[0][:, None] == text_group[None, :], 1.0, -1.0).astype(
        jnp.float32
    )
    margin = label_sign * (logit_scale * cosine + logit_bias)
    slopes = (-label_sign * jax.nn.sigmoid(-margin)).astype(jnp.bfloat16)
    update = lax.dot_general(
        slopes, img_piece, (((0,), (0,)), ((), ())), preferred_element_type=jnp.float32
    )
    grad_txt = logit_scale * update
    grad_img, local_sums = caption_side
    totals = lax.psum(local_sums, "dev")
    loss = totals[0] / pairs
    grad_scale = logit_scale * totals[1] / pairs
    grad_bias = totals[2] / pairs
    grad_images = backward_rows(grad_img, img_unit, img_length, image_head)
    grad_texts = backward_rows(grad_txt, txt_unit, txt_length, text_head)
    return (loss, grad_images, grad_texts, grad_scale, grad_bias)


def solution(mesh):
    placed = (P("dev", None), P("dev", None), P(), P(), P(), P(), P("dev"), P("dev"))
    return jax.shard_map(
        on_device,
        mesh=mesh,
        in_specs=placed,
        out_specs=(P(), P("dev", None), P("dev", None), P(), P()),
        check_vma=False,
    )
```

profile of v0, /device:TPU:14, one launch (start us, length us, event | category | flops | bytes accessed | tf_op | source)
XLA Modules:
  0.0 142.6 jit_solution(6440908995798048725)
XLA Ops:
  0.6 0.0 copy-start
  0.6 0.0 copy-start.2
  0.7 1.9 %multiply_reduce_fusion.3 = (f32[12]{0:T(128)S(1)}, f32[12,640]{1,0:T(8,128)S(1)}) fusion(bf16[12,1152]{1,0:T(8,128)(2,1)} %param.8, bf16[1152,640]{1,0:T(8,128)(2,1)} %param.10), kind=kOutput, calls=%fused_computation.22 | convolution fusion | flops 17710068 | bytes 1532976 | tf_op jit(solution)/shard_map/dot_general | solution.py:27
  2.6 0.0 copy-start.3
  2.6 0.0 copy-done
  2.6 0.0 copy-done.2
  2.6 0.4 multiply_reduce_fusion.2
  3.1 0.0 copy-start.5
  3.1 0.1 convert_bitcast_fusion
  3.2 0.4 copy-done.5
  3.6 0.0 copy-done.3
  3.7 31.5 %all_gather.7 = bf16[2,384,640]{2,0,1:T(2,128)(2,1)S(1)} all-gather(bf16[2,12,640]{2,0,1:T(2,128)(2,1)S(1)} %copy.17), channel_id=1, replica_groups=mesh['dev'=32] {'dev'}, dimensions={1}, use_global_device_ids=true | all-gather | bytes 1013760 | tf_op jit(solution)/shard_map/all_gather | solution.py:38
  35.2 1.4 fusion.30
  37.9 0.0 copy-done.7
  37.9 0.0 copy-done.8
  38.0 39.9 %all-gather = s32[32,12,2]{1,2,0:T(2,128)S(1)} all-gather(s32[1,12,2]{1,2,0:T(2,128)S(1)} %add_bitcast_fusion), channel_id=1, replica_groups=mesh['dev'=32] {'dev'}, dimensions={0}, use_global_device_ids=true | all-gather | bytes 3168 | tf_op jit(solution)/shard_map/all_gather | solution.py:39
  77.8 0.7 reshape.32
  78.5 0.8 slice_reduce_fusion
  79.3 0.0 copy-start.4
  79.3 0.0 copy-start.9
  79.3 2.0 %multiply_reduce_fusion = (f32[12]{0:T(128)S(1)}, f32[12,640]{1,0:T(8,128)}) fusion(f32[12,640]{1,0:T(8,128)S(1)} %get-tuple-element.16, f32[12]{0:T(128)} %copy-done.5, bf16[1,384,640]{2,0,1:T(2,128)(2,1)S(1)} %get-tuple-element.10, f32[]{:T(128)S(6)} %copy.37, f32[]{:T(128)S(6)} %exp.13, s32[384]{0:T(512)S(1)} %get-tuple-element.8, s32[12]{0:T(128)} %param.15), kind=kOutput, calls=%fused_computation.18 | convolution fusion | flops 11888628 | bytes 554648 | tf_op jit(solution)/shard_map/dot_general | solution.py:65
  81.3 0.0 copy-done.6
  81.3 0.0 copy-start.1
  81.3 2.0 %convolution_convert_fusion = bf16[12,1152]{1,0:T(8,128)(2,1)} fusion(bf16[1152,640]{1,0:T(8,128)(2,1)S(1)} %copy-done, f32[12,640]{1,0:T(8,128)} %get-tuple-element.23, f32[12]{0:T(128)S(1)} %get-tuple-element.22, f32[12]{0:T(128)S(1)} %copy-done.6, f32[12,640]{1,0:T(8,128)S(1)} %get-tuple-element.16), kind=kOutput, calls=%fused_computation | convolution fusion | flops 17746944 | bytes 1563744 | tf_op jit(solution)/shard_map/dot_general | solution.py:17
  83.3 0.0 copy-done.4
  83.3 0.0 copy-done.9
  83.3 0.9 fusion.11
  84.3 0.3 multiply_reduce_fusion.1
  84.6 1.2 convolution_convert_fusion.1
  85.8 2.0 %pad_maximum_fusion.1 = f32[3]{0:T(128)S(1)} fusion(f32[1]{0:T(128)} %bitcast.10, f32[1]{0:T(128)} %bitcast.9, f32[1]{0:T(128)} %bitcast.8), kind=kLoop, calls=%fused_computation.51 | loop fusion | flops 6 | bytes 24 | tf_op jit(solution)/shard_map/stack | solution.py:52
  87.8 48.9 %psum.7 = f32[3]{0:T(128)S(1)} all-reduce(f32[3]{0:T(128)S(1)} %pad_maximum_fusion.1), channel_id=1, replica_groups=mesh['dev'=32] {'dev'}, use_global_device_ids=true, to_apply=%region_5.6 | all-reduce | flops 3 | bytes 24 | tf_op jit(solution)/shard_map/psum | solution.py:70
  136.7 0.6 fusion.31
  (10 shorter events, 0.1 us)
Async XLA Ops:
  0.6 2.0 %copy-start = (bf16[1152,640]{1,0:T(8,128)(2,1)S(1)}, bf16[1152,640]{1,0:T(8,128)(2,1)}, u32[]{:S(2)}) copy-start(bf16[1152,640]{1,0:T(8,128)(2,1)} %param.11) | copy-start | bytes 4423684
  0.6 2.0 %copy-start.2 = (bf16[12,1152]{1,0:T(8,128)(2,1)S(1)}, bf16[12,1152]{1,0:T(8,128)(2,1)}, u32[]{:S(2)}) copy-start(bf16[12,1152]{1,0:T(8,128)(2,1)} %param.9) | copy-start | bytes 82948
  2.6 1.0 copy-start.3
  3.1 0.5 copy-start.5
  35.2 2.7 %copy-start.7 = (s32[12]{0:T(128)S(1)}, s32[12]{0:T(128)}, u32[]{:S(2)}) copy-start(s32[12]{0:T(128)} %param.15) | copy-start | bytes 148
  35.2 2.7 %copy-start.8 = (s32[12]{0:T(128)S(1)}, s32[12]{0:T(128)}, u32[]{:S(2)}) copy-start(s32[12]{0:T(128)} %param.14) | copy-start | bytes 148
  78.5 2.8 %copy-start.6 = (f32[12]{0:T(128)S(1)}, f32[12]{0:T(128)}, u32[]{:S(2)}) copy-start(f32[12]{0:T(128)} %copy-done.5) | copy-start | bytes 148
  79.3 4.0 %copy-start.4 = (f32[12]{0:T(128)S(1)}, f32[12]{0:T(128)}, u32[]{:S(2)}) copy-start(f32[12]{0:T(128)} %copy-done.3) | copy-start | bytes 148
  79.3 4.0 %copy-start.9 = (s32[12]{0:T(128)S(1)}, s32[12]{0:T(128)}, u32[]{:S(2)}) copy-start(s32[12]{0:T(128)} %param.14) | copy-start | bytes 148
  81.3 3.3 %copy-start.1 = (bf16[1152,640]{1,0:T(8,128)(2,1)S(1)}, bf16[1152,640]{1,0:T(8,128)(2,1)}, u32[]{:S(2)}) copy-start(bf16[1152,640]{1,0:T(8,128)(2,1)} %param.10) | copy-start | bytes 4423684
where the time goes:
time: 143 us
  blocking collectives  120 us (84%)
  matrix products  8.77 us (6%)
  between operations  7.46 us (5%)
  local copies, waits for them, and re-layouts  3.95 us (3%)
  other arithmetic  2.13 us (1%)
    psum x1, blocking collectives, on_device(): totals = lax.psum(local_sums, 'dev')  48.9 us
    all_gather x1, blocking collectives, on_device(): id_piece = lax.all_gather(stacked_ids, 'dev', axis=1, tiled=True)  39.9 us
    all_gather x1, blocking collectives, on_device(): emb_piece = lax.all_gather(stacked_emb, 'dev', axis=1, tiled=True)  31.5 us
    dot_general x2, matrix products, backward_rows(): lax.dot_general(grad_proj, weights, (((1,), (1,)), ((), ())), preferred_e...  3.2 us

commit v1 on v0

--- a/solution.py
+++ b/solution.py
@@ -67,7 +67,13 @@
     )
     grad_txt = logit_scale * update
     grad_img, local_sums = caption_side
-    totals = lax.psum(local_sums, "dev")
+    slots = lax.axis_size("dev")
+    totals = local_sums
+    for dev in [
+        [(dev_j, dev_j ^ b) for dev_j in range(slots)] for b in (1, 2, 4, 8, 16) if b < slots
+    ]:
+        inter = lax.ppermute(totals, axis_name="dev", perm=dev)
+        totals = totals + inter
     loss = totals[0] / pairs
     grad_scale = logit_scale * totals[1] / pairs
     grad_bias = totals[2] / pairs

time: 143 us -> 123 us (0.86)
  the two profiles are of different devices: /device:TPU:14 before, /device:TPU:0 now
where the time goes in v1:
time: 123 us
  blocking collectives  82.8 us (67%)
  waiting for transfers between devices  13.5 us (11%)
  matrix products  8.16 us (7%)
  between operations  7.44 us (6%)
  other arithmetic  6.18 us (5%)
  local copies, waits for them, and re-layouts  2.94 us (2%)
  starting transfers between devices  2.05 us (2%)
    all_gather x1, blocking collectives, on_device(): emb_piece = lax.all_gather(stacked_emb, 'dev', axis=1, tiled=True)  46 us
    all_gather x1, blocking collectives, on_device(): id_piece = lax.all_gather(stacked_ids, 'dev', axis=1, tiled=True)  36.7 us
    ppermute x5, waiting for transfers between devices, on_device(): inter = lax.ppermute(totals, axis_name='dev', perm=dev)  13.5 us
    add x5, other arithmetic, on_device(): totals = totals + inter  4.04 us
  transfers between devices with their start and end apart: 5, of which 4 were waited for; matrix products, arithmetic and copies ran while one was open for 4% of the time, Pallas kernels for 0%

profile of v1, /device:TPU:0, one launch (start us, length us, event | category | flops | bytes accessed | tf_op | source)
XLA Modules:
  0.0 123.0 jit_solution(8556047229400768515)
XLA Ops:
  0.6 0.0 copy-start
  0.6 0.0 copy-start.2
  0.7 1.9 %multiply_reduce_fusion.3 = (f32[12]{0:T(128)S(1)}, f32[12,640]{1,0:T(8,128)S(1)}) fusion(bf16[12,1152]{1,0:T(8,128)(2,1)} %param.8, bf16[1152,640]{1,0:T(8,128)(2,1)} %param.10), kind=kOutput, calls=%fused_computation.22 | convolution fusion | flops 17710068 | bytes 1532976 | tf_op jit(solution)/shard_map/dot_general | solution.py:27
  2.6 0.0 copy-done
  2.6 0.0 copy-done.2
  2.6 0.4 multiply_reduce_fusion.2
  3.1 0.1 convert_bitcast_fusion
  3.2 46.0 %all_gather.7 = bf16[2,384,640]{2,0,1:T(2,128)(2,1)S(1)} all-gather(bf16[2,12,640]{2,0,1:T(2,128)(2,1)S(1)} %copy.17), channel_id=1, replica_groups=mesh['dev'=32] {'dev'}, dimensions={1}, use_global_device_ids=true | all-gather | bytes 1013760 | tf_op jit(solution)/shard_map/all_gather | solution.py:38
  49.2 2.2 %fusion.30 = (bf16[1,384,640]{2,0,1:T(2,128)(2,1)}, bf16[1,384,640]{2,0,1:T(2,128)(2,1)S(1)}) fusion(bf16[2,384,640]{2,0,1:T(2,128)(2,1)S(1)} %all_gather.7), kind=kLoop, calls=%fused_computation.57 | loop fusion | bytes 1966080 | tf_op jit(solution)/shard_map/slice | solution.py:56
  52.8 36.7 %all-gather = s32[32,12,2]{1,2,0:T(2,128)S(1)} all-gather(s32[1,12,2]{1,2,0:T(2,128)S(1)} %add_bitcast_fusion), channel_id=1, replica_groups=mesh['dev'=32] {'dev'}, dimensions={0}, use_global_device_ids=true | all-gather | bytes 3168 | tf_op jit(solution)/shard_map/all_gather | solution.py:39
  89.5 0.1 reshape.32
  89.6 0.9 fusion.11
  90.6 2.0 %pad_maximum_fusion.1 = f32[3]{0:T(128)S(1)} fusion(f32[1]{0:T(128)} %bitcast.10, f32[1]{0:T(128)} %bitcast.9, f32[1]{0:T(128)} %bitcast.8), kind=kLoop, calls=%fused_computation.51 | loop fusion | flops 6 | bytes 24 | tf_op jit(solution)/shard_map/stack | solution.py:52
  92.6 0.3 collective-permute-start
  92.9 0.3 multiply_reduce_fusion.1
  93.3 0.0 copy-start.1
  93.3 2.2 %multiply_reduce_fusion = (f32[12]{0:T(128)S(1)}, f32[12,640]{1,0:T(8,128)S(1)}) fusion(f32[12,640]{1,0:T(8,128)S(1)} %get-tuple-element.16, f32[12]{0:T(128)S(1)} %add_sqrt_fusion, bf16[1,384,640]{2,0,1:T(2,128)(2,1)} %get-tuple-element.10, f32[]{:T(128)S(6)} %copy.37, f32[]{:T(128)S(6)} %exp.13, s32[384]{0:T(512)S(1)} %get-tuple-element.8, ...), kind=kOutput, calls=%fused_computation.18 | convolution fusion | flops 11888628 | bytes 554648 | tf_op jit(solution)/shard_map/dot_general | solution.py:65
  95.5 1.2 convolution_convert_fusion
  96.7 0.0 copy-done.1
  96.7 1.2 convolution_convert_fusion.1
  97.8 0.0 collective-permute-done
  97.8 2.0 %fusion.40 = f32[3]{0:T(128)S(1)} fusion(f32[3]{0:T(128)S(1)} %collective-permute-done, f32[1]{0:T(128)} %bitcast.10, f32[1]{0:T(128)} %bitcast.9, f32[1]{0:T(128)} %bitcast.8), kind=kLoop, calls=%fused_computation.59 | loop fusion | flops 9 | bytes 36 | tf_op jit(solution)/shard_map/add | solution.py:76
  99.9 1.7 %collective-permute-start.1 = (f32[3]{0:T(128)S(1)}, f32[3]{0:T(128)S(1)}, u32[]{:S(2)}, u32[]{:S(2)}) collective-permute-start(f32[3]{0:T(128)S(1)} %fusion.40), channel_id=1, source_target_pairs={{0,2},{1,3},{2,0},{3,1},{4,6},{5,7},{6,4},{7,5},{8,10},{9,11},{10,... | collective-permute-start | bytes 44 | tf_op jit(solution)/shard_map/ppermute | solution.py:75
  101.5 1.9 %collective-permute-done.1 = f32[3]{0:T(128)S(1)} collective-permute-done((f32[3]{0:T(128)S(1)}, f32[3]{0:T(128)S(1)}, u32[]{:S(2)}, u32[]{:S(2)}) %collective-permute-start.1) | collective-permute-done | bytes 44 | tf_op jit(solution)/shard_map/ppermute | solution.py:75
  103.4 2.0 %fusion.41 = f32[3]{0:T(128)S(1)} fusion(f32[3]{0:T(128)S(1)} %collective-permute-done.1, f32[3]{0:T(128)S(1)} %collective-permute-done, f32[1]{0:T(128)} %bitcast.10, f32[1]{0:T(128)} %bitcast.9, f32[1]{0:T(128)} %bitcast.8), kind=kLoop, calls=%fused_computation.60 | loop fusion | flops 12 | bytes 48 | tf_op jit(solution)/shard_map/add | solution.py:76
  105.5 0.0 collective-permute-start.2
  105.5 3.6 %collective-permute-done.2 = f32[3]{0:T(128)S(1)} collective-permute-done((f32[3]{0:T(128)S(1)}, f32[3]{0:T(128)S(1)}, u32[]{:S(2)}, u32[]{:S(2)}) %collective-permute-start.2) | collective-permute-done | bytes 44 | tf_op jit(solution)/shard_map/ppermute | solution.py:75
  109.0 0.0 collective-permute-start.3
  109.0 3.6 %collective-permute-done.3 = f32[3]{0:T(128)S(1)} collective-permute-done((f32[3]{0:T(128)S(1)}, f32[3]{0:T(128)S(1)}, u32[]{:S(2)}, u32[]{:S(2)}) %collective-permute-start.3) | collective-permute-done | bytes 44 | tf_op jit(solution)/shard_map/ppermute | solution.py:75
  112.6 0.0 collective-permute-start.4
  112.6 4.5 %collective-permute-done.4 = f32[3]{0:T(128)S(1)} collective-permute-done((f32[3]{0:T(128)S(1)}, f32[3]{0:T(128)S(1)}, u32[]{:S(2)}, u32[]{:S(2)}) %collective-permute-start.4) | collective-permute-done | bytes 44 | tf_op jit(solution)/shard_map/ppermute | solution.py:75
  117.1 0.6 fusion.31
  (14 shorter events, 0.1 us)
Async XLA Ops:
  0.6 2.0 %copy-start = (bf16[1152,640]{1,0:T(8,128)(2,1)S(1)}, bf16[1152,640]{1,0:T(8,128)(2,1)}, u32[]{:S(2)}) copy-start(bf16[1152,640]{1,0:T(8,128)(2,1)} %param.11) | copy-start | bytes 4423684
  0.6 2.0 %copy-start.2 = (bf16[12,1152]{1,0:T(8,128)(2,1)S(1)}, bf16[12,1152]{1,0:T(8,128)(2,1)}, u32[]{:S(2)}) copy-start(bf16[12,1152]{1,0:T(8,128)(2,1)} %param.9) | copy-start | bytes 82948
  49.2 3.5 %copy-start.3 = (s32[12]{0:T(128)S(1)}, s32[12]{0:T(128)}, u32[]{:S(2)}) copy-start(s32[12]{0:T(128)} %param.14) | copy-start | bytes 148
  49.2 3.5 %copy-start.4 = (s32[12]{0:T(128)S(1)}, s32[12]{0:T(128)}, u32[]{:S(2)}) copy-start(s32[12]{0:T(128)} %param.15) | copy-start | bytes 148
  92.6 5.3 %collective-permute-start = (f32[3]{0:T(128)S(1)}, f32[3]{0:T(128)S(1)}, u32[]{:S(2)}, u32[]{:S(2)}) collective-permute-start(f32[3]{0:T(128)S(1)} %pad_maximum_fusion.1), channel_id=1, source_target_pairs={{0,1},{1,0},{2,3},{3,2},{4,5},{5,4},{6,7},{7,6},{8,9},{9,8},{10,11... | collective-permute-start | bytes 44 | tf_op jit(solution)/shard_map/ppermute | solution.py:75
  93.3 3.4 %copy-start.1 = (bf16[1152,640]{1,0:T(8,128)(2,1)S(1)}, bf16[1152,640]{1,0:T(8,128)(2,1)}, u32[]{:S(2)}) copy-start(bf16[1152,640]{1,0:T(8,128)(2,1)} %param.10) | copy-start | bytes 4423684
  99.9 3.6 %collective-permute-start.1 = (f32[3]{0:T(128)S(1)}, f32[3]{0:T(128)S(1)}, u32[]{:S(2)}, u32[]{:S(2)}) collective-permute-start(f32[3]{0:T(128)S(1)} %fusion.40), channel_id=1, source_target_pairs={{0,2},{1,3},{2,0},{3,1},{4,6},{5,7},{6,4},{7,5},{8,10},{9,11},{10,... | collective-permute-start | bytes 44 | tf_op jit(solution)/shard_map/ppermute | solution.py:75
  105.5 3.6 %collective-permute-start.2 = (f32[3]{0:T(128)S(1)}, f32[3]{0:T(128)S(1)}, u32[]{:S(2)}, u32[]{:S(2)}) collective-permute-start(f32[3]{0:T(128)S(1)} %fusion.41), channel_id=1, source_target_pairs={{0,4},{1,5},{2,6},{3,7},{4,0},{5,1},{6,2},{7,3},{8,12},{9,13},{10,... | collective-permute-start | bytes 44 | tf_op jit(solution)/shard_map/ppermute | solution.py:75
  109.0 3.6 %collective-permute-start.3 = (f32[3]{0:T(128)S(1)}, f32[3]{0:T(128)S(1)}, u32[]{:S(2)}, u32[]{:S(2)}) collective-permute-start(f32[3]{0:T(128)S(1)} %add.61), channel_id=1, source_target_pairs={{0,8},{1,9},{2,10},{3,11},{4,12},{5,13},{6,14},{7,15},{8,0},{9,1},... | collective-permute-start | bytes 44 | tf_op jit(solution)/shard_map/ppermute | solution.py:75
  112.6 4.5 %collective-permute-start.4 = (f32[3]{0:T(128)S(1)}, f32[3]{0:T(128)S(1)}, u32[]{:S(2)}, u32[]{:S(2)}) collective-permute-start(f32[3]{0:T(128)S(1)} %add.62), channel_id=1, source_target_pairs={{0,16},{1,17},{2,18},{3,19},{4,20},{5,21},{6,22},{7,23},{8,24},{9,... | collective-permute-start | bytes 44 | tf_op jit(solution)/shard_map/ppermute | solution.py:75
